TPU v7x, 32 devices: a whole 2x2x4 slice. The times are simulated.
32 devices in a mesh: section: 4 (over x, core), tensor: 4 (over z), dp: 2 (over y).
Axes of the slice: x: 2, y: 2, z: 4, core: 2. Of those that a mesh axis runs over, the one named last changes fastest.
Arguments:
- layer_in: bfloat16 [2, 2, 4, 2, 128, 2560], P(None, None, 'section', 'dp', 'tensor'), may hold values from -6 to 6
- carry_in: bfloat16 [2, 4, 2, 128, 2560], P(None, 'section', 'dp', 'tensor'), may hold values from -6 to 6
- top_grad: bfloat16 [1, 2, 128, 2560], P(None, 'dp', 'tensor'), may hold values from -6 to 6
- w_qkv: bfloat16 [2, 4, 2560, 2560], P(None, 'section', None, 'tensor'), may hold values from -1 to 1
- w_out: bfloat16 [2, 4, 2048, 2560], P(None, 'section', 'tensor'), may hold values from -0.125 to 0.125
- gain: float32 [2, 4, 2560], P(None, 'section'), may hold values from 0.5 to 1.5
Outputs:
- unit_grads: bfloat16 [2, 2, 4, 2, 128, 2560], P(None, None, 'section', 'dp', 'tensor')
- grad_qkv: bfloat16 [2, 4, 2560, 2560], P(None, 'section', 'dp', 'tensor')
- grad_out: bfloat16 [2, 4, 2048, 2560], P(None, 'section', ('tensor', 'dp'))
- grad_gain: float32 [2, 4, 2560], P(None, 'section')
All inputs are finite; a program needn't handle non-finite values.
Results may differ from a plain program's by a relative error of at most 0.022.
The roundings to bfloat16 on the way count: a program that leaves them out, or rounds other values in their place, can miss the bound.
Values may be sent and summed in bfloat16 or wider, within the bound.
A program may use at most 128 MiB of HBM per device.

v0:
```python
import math
import jax
import jax.numpy as jnp
from jax import lax
from jax.sharding import PartitionSpec as P

KV = 4
HD = 64
GROUP = 8
epsilon = 1e-06
rope_base = 1000000.0


def from_behind(value, axis, steps):
    count = lax.axis_size(axis)
    first, last = (max(0, -steps), min(count, count - steps))
    return lax.ppermute(value, axis, [(source, source + steps) for source in range(first, last)])


def rope_tables(length, head_width):
    half_width = head_width // 2
    exponent = jnp.arange(half_width, dtype=jnp.float32) * (2.0 / head_width)
    frequency = rope_base ** (-exponent)
    angle = jnp.arange(length, dtype=jnp.float32)[:, None] * frequency[None, :]
    return (jnp.cos(angle), jnp.sin(angle))


def rotate(values, cosine_table, sine_table, direction):
    half_width = values.shape[-1] // 2
    table_shape = (values.shape[0],) + (1,) * (values.ndim - 2) + (half_width,)
    cosine = cosine_table.reshape(table_shape)
    sine_part = direction * sine_table.reshape(table_shape)
    lower_half = values[..., :half_width]
    upper_half = values[..., half_width:]
    return jnp.concatenate(
        [
            lower_half * cosine - upper_half * sine_part,
            upper_half * cosine + lower_half * sine_part,
        ],
        axis=-1,
    )


def local(layer_in, carry_in, top_grad, w_qkv, w_out, gain):
    ticks = layer_in.shape[0]
    own_rows = layer_in.shape[4]
    length = own_rows * lax.axis_size("tensor")
    kv_local = KV // lax.axis_size("tensor")
    section_index = lax.axis_index("section")
    at_first = section_index == 0
    at_last = section_index == lax.axis_size("section") - 1
    cosine_table, sine_table = rope_tables(length, HD)
    score_scale = 1.0 / math.sqrt(HD)
    causal_mask = jnp.arange(length)[:, None] >= jnp.arange(length)[None, :]
    layer_rows = layer_in[:, :, 0, 0]
    carried = carry_in[:, 0, 0]
    fresh_grads = top_grad[:, 0]
    weight_qkv = w_qkv[:, 0]
    weight_out = w_out[:, 0]
    gain_rows = gain[:, 0]
    contract_rows = (((0,), (0,)), ((), ()))
    contract_cols = (((1,), (1,)), ((), ()))
    qkv_sums = [
        jnp.zeros(weight_qkv.shape[1:], jnp.float32),
        jnp.zeros(weight_qkv.shape[1:], jnp.float32),
    ]
    out_sums = [
        jnp.zeros(weight_out.shape[1:], jnp.float32),
        jnp.zeros(weight_out.shape[1:], jnp.float32),
    ]
    gain_totals = [
        jnp.zeros(gain_rows.shape[1:], jnp.float32),
        jnp.zeros(gain_rows.shape[1:], jnp.float32),
    ]

    def apply_weights(member, stored):
        normed, grad_full, attended, grad_projected = stored
        qkv_sums[member] = qkv_sums[member] + lax.dot_general(
            normed, grad_projected, contract_rows, preferred_element_type=jnp.float32
        )
        out_sums[member] = out_sums[member] + lax.dot_general(
            attended, grad_full, contract_rows, preferred_element_type=jnp.float32
        )

    inputs = [carried[0], carried[1]]
    per_tick = []
    for position in range(ticks):
        outcome = [None, None]
        pending_members = []
        pending_saved = []
        for member in (1, 0):
            layer_part = layer_rows[position, member]
            grad_output = inputs[member]
            inputs_float = layer_part.astype(jnp.float32)
            inverse = lax.rsqrt(
                jnp.mean(inputs_float * inputs_float, axis=-1, keepdims=True) + epsilon
            )
            unit_rows = inputs_float * inverse
            normed_own = (unit_rows * gain_rows[member]).astype(jnp.bfloat16)
            input_normed = lax.all_gather(normed_own, "tensor", axis=0, tiled=True)
            input_grad_full = lax.all_gather(grad_output, "tensor", axis=0, tiled=True)
            projected = jnp.dot(
                input_normed, weight_qkv[member], preferred_element_type=jnp.float32
            )
            projected = projected.reshape(length, kv_local, GROUP + 2, HD)
            query_rot = rotate(projected[:, :, :GROUP], cosine_table, sine_table, 1.0).astype(
                jnp.bfloat16
            )
            key_rot = rotate(projected[:, :, GROUP], cosine_table, sine_table, 1.0).astype(
                jnp.bfloat16
            )
            value_rows = projected[:, :, GROUP + 1].astype(jnp.bfloat16)
            scores = (
                jnp.einsum("tkgd,ukd->kgtu", query_rot, key_rot, preferred_element_type=jnp.float32)
                * score_scale
            )
            scores = jnp.where(causal_mask, scores, -1e30)
            exponentials = jnp.exp(scores - jnp.max(scores, axis=-1, keepdims=True))
            softmax_rows = exponentials / jnp.sum(exponentials, axis=-1, keepdims=True)
            softmax_low = softmax_rows.astype(jnp.bfloat16)
            input_attended = jnp.einsum(
                "kgtu,ukd->tkgd", softmax_low, value_rows, preferred_element_type=jnp.float32
            )
            input_attended = input_attended.astype(jnp.bfloat16).reshape(
                length, kv_local * GROUP * HD
            )
            grad_attended = lax.dot_general(
                input_grad_full,
                weight_out[member],
                contract_cols,
                preferred_element_type=jnp.float32,
            ).astype(jnp.bfloat16)
            grad_heads = grad_attended.reshape(length, kv_local, GROUP, HD)
            grad_softmax = jnp.einsum(
                "tkgd,ukd->kgtu", grad_heads, value_rows, preferred_element_type=jnp.float32
            )
            row_total = jnp.sum(softmax_rows * grad_softmax, axis=-1, keepdims=True)
            grad_scores = (softmax_rows * (grad_softmax - row_total) * score_scale).astype(
                jnp.bfloat16
            )
            grad_value = jnp.einsum(
                "kgtu,tkgd->ukd", softmax_low, grad_heads, preferred_element_type=jnp.float32
            )
            grad_query = rotate(
                jnp.einsum(
                    "kgtu,ukd->tkgd", grad_scores, key_rot, preferred_element_type=jnp.float32
                ),
                cosine_table,
                sine_table,
                -1.0,
            )
            grad_key = rotate(
                jnp.einsum(
                    "kgtu,tkgd->ukd", grad_scores, query_rot, preferred_element_type=jnp.float32
                ),
                cosine_table,
                sine_table,
                -1.0,
            )
            input_grad_projected = jnp.concatenate(
                [grad_query, grad_key[:, :, None], grad_value[:, :, None]], axis=2
            )
            input_grad_projected = input_grad_projected.reshape(
                length, kv_local * (GROUP + 2) * HD
            ).astype(jnp.bfloat16)
            grad_normed = lax.psum_scatter(
                lax.dot_general(
                    input_grad_projected,
                    weight_qkv[member],
                    contract_cols,
                    preferred_element_type=jnp.float32,
                ).astype(jnp.bfloat16),
                "tensor",
                scatter_dimension=0,
                tiled=True,
            ).astype(jnp.float32)
            grad_unit = grad_normed * gain_rows[member]
            grad_rows = inverse * (
                grad_unit - unit_rows * jnp.mean(grad_unit * unit_rows, axis=-1, keepdims=True)
            )
            grad_input = (grad_output.astype(jnp.float32) + grad_rows).astype(jnp.bfloat16)
            grad_scale = jnp.sum(grad_normed * unit_rows, axis=0)
            grad_input, stored, grad_scale = (
                grad_input,
                (input_normed, input_grad_full, input_attended, input_grad_projected),
                grad_scale,
            )
            outcome[member] = grad_input
            gain_totals[member] = gain_totals[member] + grad_scale
            pending_members.append(member)
            pending_saved.append(stored)
        if position + 1 < ticks:
            upward = from_behind(outcome[1], "section", 1)
            downward = from_behind(outcome[0], "section", -1)
            pending_saved, upward, downward = lax.optimization_barrier(
                (pending_saved, upward, downward)
            )
            inputs = [
                jnp.where(at_last, outcome[1], downward),
                jnp.where(at_first, fresh_grads[position], upward),
            ]
        for member, stored in zip(pending_members, pending_saved):
            apply_weights(member, stored)
        per_tick.append(jnp.stack(outcome))
    grad_qkv_all, grad_out_all = (
        lax.psum_scatter(
            jnp.stack(qkv_sums).astype(jnp.bfloat16), "dp", scatter_dimension=1, tiled=True
        ).astype(jnp.float32),
        lax.psum_scatter(
            jnp.stack(out_sums).astype(jnp.bfloat16), "dp", scatter_dimension=1, tiled=True
        ).astype(jnp.float32),
    )
    gain_total = lax.psum(jnp.stack(gain_totals), ("tensor", "dp"))
    unit_grads = jnp.stack(per_tick)[:, :, None, None]
    return (
        unit_grads,
        grad_qkv_all.astype(jnp.bfloat16)[:, None],
        grad_out_all.astype(jnp.bfloat16)[:, None],
        gain_total[:, None],
    )


def solution(mesh):
    in_specs = (
        P(None, None, "section", "dp", "tensor", None),
        P(None, "section", "dp", "tensor", None),
        P(None, "dp", "tensor", None),
        P(None, "section", None, "tensor"),
        P(None, "section", "tensor", None),
        P(None, "section", None),
    )
    out_specs = (
        P(None, None, "section", "dp", "tensor", None),
        P(None, "section", "dp", "tensor"),
        P(None, "section", ("tensor", "dp"), None),
        P(None, "section", None),
    )
    return jax.shard_map(local, mesh=mesh, in_specs=in_specs, out_specs=out_specs, check_vma=False)
```

profile of v0, /device:TPU:0, one launch (start us, length us, event | category | flops | bytes accessed | tf_op | source)
XLA Modules:
  0.0 479.4 jit_solution(15156333436391977317)
XLA Ops:
  11.8 19.7 %all-gather = bf16[1,1,1,128,2560]{4,3,2,1,0:T(8,128)(2,1)S(1)} all-gather(bf16[1,1,1,32,2560]{4,3,2,1,0:T(8,128)(2,1)S(1)} %get-tuple-element.68), channel_id=2, replica_groups=mesh['section'=4,'tensor'=4,'dp'=2] {'tensor'}, dimensions={3}, use_global_device_ids=true | all-gather | bytes 819200 | tf_op jit(solution)/shard_map/all_gather | solution.py:101
  32.3 2.7 fusion.32
  35.4 17.5 %all_gather.24 = bf16[128,2560]{1,0:T(8,128)(2,1)} all-gather(bf16[32,2560]{1,0:T(8,128)(2,1)S(1)} %get-tuple-element.58), channel_id=1, replica_groups=mesh['section'=4,'tensor'=4,'dp'=2] {'tensor'}, dimensions={0}, use_global_device_ids=true | all-gather | bytes 819200 | tf_op jit(solution)/shard_map/all_gather | solution.py:100
  52.9 16.7 %all_gather.26 = bf16[128,2560]{1,0:T(8,128)(2,1)} all-gather(bf16[32,2560]{1,0:T(8,128)(2,1)S(1)} %get-tuple-element.59), channel_id=1, replica_groups=mesh['section'=4,'tensor'=4,'dp'=2] {'tensor'}, dimensions={0}, use_global_device_ids=true | all-gather | bytes 819200 | tf_op jit(solution)/shard_map/all_gather | solution.py:100
  69.6 6.2 %slice_bitcast_fusion.1 = (bf16[640,2560]{0,1:T(8,128)(2,1)}, bf16[640,2560]{0,1:T(8,128)(2,1)}) fusion(bf16[2,1,2560,640]{3,2,1,0:T(8,128)(2,1)} %param.9), kind=kLoop, calls=%fused_computation.30 | loop fusion | bytes 13107200 | tf_op jit(solution)/shard_map/dot_general | solution.py:102
  75.9 4.0 copy.39
  79.9 2.1 convolution_bitcast_fusion.7
  82.7 5.7 %copy.44 = bf16[640,2560]{1,0:T(8,128)(2,1)} copy(bf16[640,2560]{0,1:T(8,128)(2,1)} %get-tuple-element.51) | data formatting | bytes 6553600 | tf_op jit(solution)/shard_map/dot_general | solution.py:102
  88.4 3.2 convolution_bitcast_fusion.6
  95.4 15.2 %all-gather.1 = bf16[1,1,1,128,2560]{4,3,2,1,0:T(8,128)(2,1)S(1)} all-gather(bf16[1,1,1,32,2560]{4,3,2,1,0:T(8,128)(2,1)S(1)} %copy-done.33), channel_id=3, replica_groups=mesh['section'=4,'tensor'=4,'dp'=2] {'tensor'}, dimensions={3}, use_global_device_ids=true | all-gather | bytes 819200 | tf_op jit(solution)/shard_map/all_gather | solution.py:101
  111.5 3.4 fusion.38
  123.0 4.0 convolution_convert_fusion.2
  129.2 4.0 convolution_convert_fusion.3
  137.2 13.4 %reduce-scatter.9.cloned.1.call-done = bf16[32,2560]{1,0:T(8,128)(2,1)} async-done(((bf16[128,2560]{1,0:T(8,128)(2,1)}), bf16[32,2560]{1,0:T(8,128)(2,1)}) %reduce-scatter.9.cloned.1.call-update) | async-done | bytes 163856 | tf_op jit(solution)/shard_map/reduce_scatter | solution.py:166
  150.5 24.1 %reduce-scatter.7.cloned.1.call-done = bf16[32,2560]{1,0:T(8,128)(2,1)} async-done(((bf16[128,2560]{1,0:T(8,128)(2,1)}), bf16[32,2560]{1,0:T(8,128)(2,1)}) %reduce-scatter.7.cloned.1.call-update) | async-done | bytes 163856 | tf_op jit(solution)/shard_map/reduce_scatter | solution.py:166
  174.7 2.3 fusion.90
  178.8 16.5 %all_gather.30 = bf16[128,2560]{1,0:T(8,128)(2,1)S(1)} all-gather(bf16[32,2560]{1,0:T(8,128)(2,1)S(1)} %get-tuple-element.54), channel_id=1, replica_groups=mesh['section'=4,'tensor'=4,'dp'=2] {'tensor'}, dimensions={0}, use_global_device_ids=true | all-gather | bytes 819200 | tf_op jit(solution)/shard_map/all_gather | solution.py:100
  196.4 15.8 %all_gather.28 = bf16[128,2560]{1,0:T(8,128)(2,1)S(1)} all-gather(bf16[32,2560]{1,0:T(8,128)(2,1)S(1)} %get-tuple-element.55), channel_id=1, replica_groups=mesh['section'=4,'tensor'=4,'dp'=2] {'tensor'}, dimensions={0}, use_global_device_ids=true | all-gather | bytes 819200 | tf_op jit(solution)/shard_map/all_gather | solution.py:100
  214.8 3.0 collective-permute-start
  221.0 17.3 %all_gather.29 = bf16[128,2560]{1,0:T(8,128)(2,1)S(1)} all-gather(bf16[32,2560]{1,0:T(8,128)(2,1)S(1)} %broadcast_select_fusion), channel_id=1, replica_groups=mesh['section'=4,'tensor'=4,'dp'=2] {'tensor'}, dimensions={0}, use_global_device_ids=true | all-gather | bytes 819200 | tf_op jit(solution)/shard_map/all_gather | solution.py:101
  244.0 16.7 %all_gather.31 = bf16[128,2560]{1,0:T(8,128)(2,1)S(1)} all-gather(bf16[32,2560]{1,0:T(8,128)(2,1)S(1)} %bitcast_select_fusion), channel_id=1, replica_groups=mesh['section'=4,'tensor'=4,'dp'=2] {'tensor'}, dimensions={0}, use_global_device_ids=true | all-gather | bytes 819200 | tf_op jit(solution)/shard_map/all_gather | solution.py:101
  261.5 3.5 fusion.41
  272.2 2.0 convolution_convert_fusion
  277.3 4.0 convolution_convert_fusion.1
  281.2 3.2 fusion.189
  284.5 3.4 fusion.3
  289.9 2.7 pad_maximum_fusion.1
  298.0 3.4 pad_maximum_fusion
  302.5 19.2 %reduce-scatter.11.cloned.1.call-done = bf16[32,2560]{1,0:T(8,128)(2,1)} async-done(((bf16[128,2560]{1,0:T(8,128)(2,1)}), bf16[32,2560]{1,0:T(8,128)(2,1)}) %reduce-scatter.11.cloned.1.call-update) | async-done | bytes 163856 | tf_op jit(solution)/shard_map/reduce_scatter | solution.py:166
  323.2 36.0 %psum.7 = f32[2,1,2560]{2,1,0:T(1,128)} all-reduce(f32[2,1,2560]{2,1,0:T(1,128)S(1)} %broadcast_in_dim.33), channel_id=1, replica_groups=mesh['section'=4,'tensor'=4,'dp'=2] {'tensor','dp'}, use_global_device_ids=true, to_apply=%region_30.31 | all-reduce | flops 5120 | bytes 40960 | tf_op jit(solution)/shard_map/psum | solution.py:213
  361.4 28.5 %reduce-scatter.17.cloned.1.call-done = bf16[2,256,2560]{2,1,0:T(8,128)(2,1)} async-done(((bf16[2,512,2560]{2,1,0:T(8,128)(2,1)}), bf16[2,256,2560]{2,1,0:T(8,128)(2,1)}) %reduce-scatter.17.cloned.1.call-update) | async-done | bytes 2621456 | tf_op jit(solution)/shard_map/reduce_scatter | solution.py:209
  389.9 82.6 %reduce-scatter.15.cloned.1.call-done = bf16[2,1280,640]{2,1,0:T(8,128)(2,1)} async-done(((bf16[2,2560,640]{2,1,0:T(8,128)(2,1)}), bf16[2,1280,640]{2,1,0:T(8,128)(2,1)}) %reduce-scatter.15.cloned.1.call-update) | async-done | bytes 3276816 | tf_op jit(solution)/shard_map/reduce_scatter | solution.py:206
  (319 shorter events, 61.7 us)
Async XLA Ops:
  7.2 28.0 %copy-start.1 = (bf16[2,2,1,1,32,2560]{5,4,3,2,1,0:T(8,128)(2,1)S(1)}, bf16[2,2,1,1,32,2560]{5,4,3,2,1,0:T(8,128)(2,1)}, u32[]{:S(2)}) copy-start(bf16[2,2,1,1,32,2560]{5,4,3,2,1,0:T(8,128)(2,1)} %param.6) | copy-start | bytes 1966084
  7.2 143.4 %reduce-scatter.9.cloned.1.call-start = ((), (), s32[]{:S(2)}) async-start(), calls=%async_computation.7 | async-start | bytes 819200 | tf_op jit(solution)/shard_map/reduce_scatter | solution.py:166
  7.2 84.4 %copy-start.88 = (f32[32]{0:T(128)}, f32[32]{0:T(128)S(1)}, u32[]{:S(2)}) copy-start(f32[32]{0:T(128)S(1)} %negate_power_fusion) | copy-start | bytes 388
  7.3 85.9 %copy-start.49 = (pred[128,128]{0,1:T(8,128)(4,1)}, pred[128,128]{0,1:T(8,128)(4,1)S(1)}, u32[]{:S(2)}) copy-start(pred[128,128]{0,1:T(8,128)(4,1)S(1)} %iota_compare_fusion) | copy-start | bytes 49156
  9.3 26.1 %copy-start.42 = (f32[2560]{0:T(1024)}, f32[2560]{0:T(1024)S(1)}, u32[]{:S(2)}) copy-start(f32[2560]{0:T(1024)S(1)} %get-tuple-element.49) | copy-start | bytes 30724
  10.1 82.3 %copy-start.45 = (f32[128,32]{0,1:T(8,128)}, f32[128,32]{0,1:T(8,128)S(1)}, u32[]{:S(2)}) copy-start(f32[128,32]{0,1:T(8,128)S(1)} %get-tuple-element.112) | copy-start | bytes 49156
  10.1 82.3 %copy-start.59 = (f32[128,32]{0,1:T(8,128)}, f32[128,32]{0,1:T(8,128)S(1)}, u32[]{:S(2)}) copy-start(f32[128,32]{0,1:T(8,128)S(1)} %get-tuple-element.111) | copy-start | bytes 49156
  35.1 58.4 %copy-start.63 = (bf16[128,512]{0,1:T(8,128)(2,1)}, bf16[128,512]{0,1:T(8,128)(2,1)S(1)}, u32[]{:S(2)}) copy-start(bf16[128,512]{0,1:T(8,128)(2,1)S(1)} %copy.40) | copy-start | bytes 393220
  35.2 40.7 %copy-start.92 = (f32[32]{0:T(128)}, f32[32]{0:T(128)S(1)}, u32[]{:S(2)}) copy-start(f32[32]{0:T(128)S(1)} %get-tuple-element.129) | copy-start | bytes 388
  35.2 40.7 %copy-start.94 = (f32[32]{0:T(128)}, f32[32]{0:T(128)S(1)}, u32[]{:S(2)}) copy-start(f32[32]{0:T(128)S(1)} %get-tuple-element.130) | copy-start | bytes 388
  127.0 47.6 %reduce-scatter.7.cloned.1.call-start = ((), (), s32[]{:S(2)}) async-start(), calls=%async_computation.6 | async-start | bytes 819200 | tf_op jit(solution)/shard_map/reduce_scatter | solution.py:166
  133.1 41.5 %copy-start.43 = (f32[2560]{0:T(1024)S(1)}, f32[2560]{0:T(1024)}, u32[]{:S(2)}) copy-start(f32[2560]{0:T(1024)} %copy-done.42) | copy-start | bytes 30724
  133.2 41.5 %copy-start.93 = (f32[32]{0:T(128)S(1)}, f32[32]{0:T(128)}, u32[]{:S(2)}) copy-start(f32[32]{0:T(128)} %copy-done.92) | copy-start | bytes 388
  133.2 41.5 %copy-start.95 = (f32[32]{0:T(128)S(1)}, f32[32]{0:T(128)}, u32[]{:S(2)}) copy-start(f32[32]{0:T(128)} %copy-done.94) | copy-start | bytes 388
  133.2 169.3 %reduce-scatter.13.cloned.1.call-start = ((), (), s32[]{:S(2)}) async-start(), calls=%async_computation.9 | async-start | bytes 819200 | tf_op jit(solution)/shard_map/reduce_scatter | solution.py:166
  174.7 20.7 %copy-start = (bf16[640,2560]{1,0:T(8,128)(2,1)S(1)}, bf16[640,2560]{1,0:T(8,128)(2,1)}, u32[]{:S(2)}) copy-start(bf16[640,2560]{1,0:T(8,128)(2,1)} %copy.44) | copy-start | bytes 9830404
  178.8 34.6 %copy-start.31 = (bf16[32,2560]{1,0:T(8,128)(2,1)}, bf16[32,2560]{1,0:T(8,128)(2,1)S(1)}, u32[]{:S(2)}) copy-start(bf16[32,2560]{1,0:T(8,128)(2,1)S(1)} %get-tuple-element.52) | copy-start | bytes 491524
  178.8 41.5 %copy-start.19 = (bf16[32,2560]{1,0:T(8,128)(2,1)}, bf16[32,2560]{1,0:T(8,128)(2,1)S(1)}, u32[]{:S(2)}) copy-start(bf16[32,2560]{1,0:T(8,128)(2,1)S(1)} %get-tuple-element.53) | copy-start | bytes 491524
  195.3 43.9 %slice-start.2 = ((s8[5242880]{0:T(1024)(128)(4,1)}), s8[1048576]{0:T(1024)(128)(4,1)S(1)}, s32[]{:S(2)}) async-start(s8[5242880]{0:T(1024)(128)(4,1)} %bitcast.493), calls=%async_computation.14 | async-start | bytes 2097152
  196.4 21.4 %copy-start.90 = (f32[32]{0:T(128)S(1)}, f32[32]{0:T(128)}, u32[]{:S(2)}) copy-start(f32[32]{0:T(128)} %copy-done.88) | copy-start | bytes 388
  196.4 21.6 %copy-start.50 = (pred[128,128]{0,1:T(8,128)(4,1)S(1)}, pred[128,128]{0,1:T(8,128)(4,1)}, u32[]{:S(2)}) copy-start(pred[128,128]{0,1:T(8,128)(4,1)} %copy-done.49) | copy-start | bytes 49156
  212.2 27.1 %slice-start.3 = ((s8[5242880]{0:T(1024)(128)(4,1)}), s8[4194304]{0:T(1024)(128)(4,1)S(1)}, s32[]{:S(2)}) async-start(s8[5242880]{0:T(1024)(128)(4,1)} %bitcast.493), calls=%async_computation.15 | async-start | bytes 8388608
  213.4 6.9 %collective-permute-start.1 = (bf16[32,2560]{1,0:T(8,128)(2,1)S(1)}, bf16[32,2560]{1,0:T(8,128)(2,1)S(1)}, u32[]{:S(2)}, u32[]{:S(2)}) collective-permute-start(bf16[32,2560]{1,0:T(8,128)(2,1)S(1)} %get-tuple-element.52), channel_id=1, source_target_pairs={{8,0},{16,8},{24,16},{9,1},{17,9},{25,17},{10,2},{18,10},{26,18},{... | collective-permute-start | bytes 491528 | tf_op jit(solution)/shard_map/ppermute | solution.py:17
  214.8 5.5 %collective-permute-start = (bf16[32,2560]{1,0:T(8,128)(2,1)S(1)}, bf16[32,2560]{1,0:T(8,128)(2,1)S(1)}, u32[]{:S(2)}, u32[]{:S(2)}) collective-permute-start(bf16[32,2560]{1,0:T(8,128)(2,1)S(1)} %get-tuple-element.53), channel_id=1, source_target_pairs={{0,8},{8,16},{16,24},{1,9},{9,17},{17,25},{2,10},{10,18},{18,26},{... | collective-permute-start | bytes 491528 | tf_op jit(solution)/shard_map/ppermute | solution.py:17
  218.4 23.0 %copy-start.84 = (f32[8,128]{1,0:T(8,128)}, f32[8,128]{1,0:T(8,128)S(1)}, u32[]{:S(2)}) copy-start(f32[8,128]{1,0:T(8,128)S(1)} %fusion.53) | copy-start | bytes 12292
  274.2 47.5 %reduce-scatter.11.cloned.1.call-start = ((), (), s32[]{:S(2)}) async-start(), calls=%async_computation.8 | async-start | bytes 819200 | tf_op jit(solution)/shard_map/reduce_scatter | solution.py:166
  284.4 105.5 %reduce-scatter.17.cloned.1.call-start = ((), (), s32[]{:S(2)}) async-start(), calls=%async_computation.11 | async-start | bytes 7864320 | tf_op jit(solution)/shard_map/reduce_scatter | solution.py:209
  292.6 179.9 %reduce-scatter.15.cloned.1.call-start = ((), (), s32[]{:S(2)}) async-start(), calls=%async_computation.10 | async-start | bytes 9830400 | tf_op jit(solution)/shard_map/reduce_scatter | solution.py:206
  301.4 21.6 %copy-start.75 = (f32[2560]{0:T(1024)S(1)}, f32[2560]{0:T(1024)}, u32[]{:S(2)}) copy-start(f32[2560]{0:T(1024)} %get-tuple-element.43) | copy-start | bytes 30724
  301.4 21.7 %copy-start.74 = (f32[2560]{0:T(1024)S(1)}, f32[2560]{0:T(1024)}, u32[]{:S(2)}) copy-start(f32[2560]{0:T(1024)} %get-tuple-element.34) | copy-start | bytes 30724
  301.5 57.7 %copy-start.22 = (bf16[32,2560]{1,0:T(8,128)(2,1)S(1)}, bf16[32,2560]{1,0:T(8,128)(2,1)}, u32[]{:S(2)}) copy-start(bf16[32,2560]{1,0:T(8,128)(2,1)} %copy-done.21) | copy-start | bytes 491524
  301.5 57.7 %copy-start.24 = (bf16[32,2560]{1,0:T(8,128)(2,1)S(1)}, bf16[32,2560]{1,0:T(8,128)(2,1)}, u32[]{:S(2)}) copy-start(bf16[32,2560]{1,0:T(8,128)(2,1)} %copy-done.23) | copy-start | bytes 491524
  (80 other events, 446.7 us)
Sparse Core Ops, SparseCore 0:
  127.1 23.3 reduce-scatter.8
  153.4 21.2 reduce-scatter.6
  274.4 23.2 reduce-scatter.12
  300.4 21.2 reduce-scatter.10
  324.4 65.4 reduce-scatter.16
  392.6 79.8 reduce-scatter.14
where the time goes:
time: 481 us; the launch traced here: 479 us
  blocking collectives  171 us (36%)
  waiting for transfers between devices  168 us (35%)
  matrix products  64 us (13%)
  local copies, waits for them, and re-layouts  32.3 us (7%)
  other arithmetic  23 us (5%)
  between operations  15.6 us (3%)
  starting transfers between devices  4.93 us (1%)
    reduce_scatter x1, waiting for transfers between devices, local(): lax.psum_scatter(jnp.stack(qkv_sums).astype(jnp.bfloat16), 'dp', scatter_...  82.6 us
    all_gather x4, blocking collectives, local(): input_grad_full = lax.all_gather(grad_output, 'tensor', axis=0, tiled=True)  68.9 us
    all_gather x4, blocking collectives, local(): input_normed = lax.all_gather(normed_own, 'tensor', axis=0, tiled=True)  66.6 us
    reduce_scatter x4, waiting for transfers between devices, local(): lax.psum_scatter(lax.dot_general(input_grad_projected, weight_qkv[member]...  56.8 us
    psum x1, blocking collectives, local(): gain_total = lax.psum(jnp.stack(gain_totals), ('tensor', 'dp'))  36 us
    reduce_scatter x1, waiting for transfers between devices, local(): lax.psum_scatter(jnp.stack(out_sums).astype(jnp.bfloat16), 'dp', scatter_...  28.5 us
    dot_general x3, local copies, waits for them, and re-layouts, local(): jnp.dot(input_normed, weight_qkv[member], preferred_element_type=jnp.floa...  15.9 us
    dot_general x4, matrix products, local(): lax.dot_general(input_grad_projected, weight_qkv[member], contract_cols,...  14 us
  transfers between devices with their start and end apart: 8, of which 5 were waited for; matrix products, arithmetic and copies ran while one was open for 8% of the time, Pallas kernels for 0%

commit v1 on v0

--- a/solution.py
+++ b/solution.py
@@ -210,7 +210,9 @@
             jnp.stack(out_sums).astype(jnp.bfloat16), "dp", scatter_dimension=1, tiled=True
         ).astype(jnp.float32),
     )
-    gain_total = lax.psum(jnp.stack(gain_totals), ("tensor", "dp"))
+    part = jnp.stack(gain_totals)
+    terms = lax.all_gather(part, ("tensor", "dp"), axis=0, tiled=False)
+    gain_total = terms.sum(axis=0)
     unit_grads = jnp.stack(per_tick)[:, :, None, None]
     return (
         unit_grads,

time: 481 us -> 482 us (level)
  waiting for transfers between devices: 168 us -> 174 us
  blocking collectives: 171 us -> 166 us
    psum x1 -> x0, blocking collectives: 36 us -> none  [local(): gain_total = lax.psum(jnp.stack(gain_totals), ('tensor', 'dp'))]
    all_gather x0 -> x1, blocking collectives: none -> 31 us  [local(): terms = lax.all_gather(part, ('tensor', 'dp'), axis=0, tiled=False)]
    reduce_scatter x1, waiting for transfers between devices: 28.5 us -> 34.1 us  [local(): lax.psum_scatter(jnp.stack(out_sums).astype(jnp.bfloat16), 'dp', scatter_...]
  transfers between devices with their start and end apart: 8 -> 8, of which waited for: 5 -> 5; matrix products, arithmetic and copies ran while one was open for 8% -> 9% of each run, Pallas kernels for 0% -> 0%
where the time goes in v1:
time: 482 us; the launch traced here: 481 us
  waiting for transfers between devices  174 us (36%)
  blocking collectives  166 us (34%)
  matrix products  64 us (13%)
  local copies, waits for them, and re-layouts  33 us (7%)
  other arithmetic  23.1 us (5%)
  between operations  15.6 us (3%)
  starting transfers between devices  4.93 us (1%)
    reduce_scatter x1, waiting for transfers between devices, local(): lax.psum_scatter(jnp.stack(qkv_sums).astype(jnp.bfloat16), 'dp', scatter_...  82.6 us
    all_gather x4, blocking collectives, local(): input_grad_full = lax.all_gather(grad_output, 'tensor', axis=0, tiled=True)  68.9 us
    all_gather x4, blocking collectives, local(): input_normed = lax.all_gather(normed_own, 'tensor', axis=0, tiled=True)  66.6 us
    reduce_scatter x4, waiting for transfers between devices, local(): lax.psum_scatter(lax.dot_general(input_grad_projected, weight_qkv[member]...  56.8 us
    reduce_scatter x1, waiting for transfers between devices, local(): lax.psum_scatter(jnp.stack(out_sums).astype(jnp.bfloat16), 'dp', scatter_...  34.1 us
    all_gather x1, blocking collectives, local(): terms = lax.all_gather(part, ('tensor', 'dp'), axis=0, tiled=False)  31 us
    dot_general x3, local copies, waits for them, and re-layouts, local(): jnp.dot(input_normed, weight_qkv[member], preferred_element_type=jnp.floa...  15.9 us
    dot_general x4, matrix products, local(): lax.dot_general(input_grad_projected, weight_qkv[member], contract_cols,...  14 us
  transfers between devices with their start and end apart: 8, of which 5 were waited for; matrix products, arithmetic and copies ran while one was open for 9% of the time, Pallas kernels for 0%

profile of v1, /device:TPU:0, one launch (start us, length us, event | category | flops | bytes accessed | tf_op | source)
XLA Modules:
  0.0 480.7 jit_solution(13351605759696971080)
XLA Ops:
  11.8 19.7 %all-gather = bf16[1,1,1,128,2560]{4,3,2,1,0:T(8,128)(2,1)S(1)} all-gather(bf16[1,1,1,32,2560]{4,3,2,1,0:T(8,128)(2,1)S(1)} %get-tuple-element.72), channel_id=2, replica_groups=mesh['section'=4,'tensor'=4,'dp'=2] {'tensor'}, dimensions={3}, use_global_device_ids=true | all-gather | bytes 819200 | tf_op jit(solution)/shard_map/all_gather | solution.py:101
  32.3 2.7 fusion.32
  35.4 17.5 %all_gather.30 = bf16[128,2560]{1,0:T(8,128)(2,1)} all-gather(bf16[32,2560]{1,0:T(8,128)(2,1)S(1)} %get-tuple-element.62), channel_id=1, replica_groups=mesh['section'=4,'tensor'=4,'dp'=2] {'tensor'}, dimensions={0}, use_global_device_ids=true | all-gather | bytes 819200 | tf_op jit(solution)/shard_map/all_gather | solution.py:100
  52.9 16.7 %all_gather.32 = bf16[128,2560]{1,0:T(8,128)(2,1)} all-gather(bf16[32,2560]{1,0:T(8,128)(2,1)S(1)} %get-tuple-element.63), channel_id=1, replica_groups=mesh['section'=4,'tensor'=4,'dp'=2] {'tensor'}, dimensions={0}, use_global_device_ids=true | all-gather | bytes 819200 | tf_op jit(solution)/shard_map/all_gather | solution.py:100
  69.6 6.2 %slice_bitcast_fusion.1 = (bf16[640,2560]{0,1:T(8,128)(2,1)}, bf16[640,2560]{0,1:T(8,128)(2,1)}) fusion(bf16[2,1,2560,640]{3,2,1,0:T(8,128)(2,1)} %param.9), kind=kLoop, calls=%fused_computation.30 | loop fusion | bytes 13107200 | tf_op jit(solution)/shard_map/dot_general | solution.py:102
  75.9 4.0 copy.64
  79.9 2.1 convolution_bitcast_fusion.7
  82.7 5.7 %copy.69 = bf16[640,2560]{1,0:T(8,128)(2,1)} copy(bf16[640,2560]{0,1:T(8,128)(2,1)} %get-tuple-element.55) | data formatting | bytes 6553600 | tf_op jit(solution)/shard_map/dot_general | solution.py:102
  88.4 3.2 convolution_bitcast_fusion.6
  95.4 15.2 %all-gather.1 = bf16[1,1,1,128,2560]{4,3,2,1,0:T(8,128)(2,1)S(1)} all-gather(bf16[1,1,1,32,2560]{4,3,2,1,0:T(8,128)(2,1)S(1)} %copy-done.33), channel_id=3, replica_groups=mesh['section'=4,'tensor'=4,'dp'=2] {'tensor'}, dimensions={3}, use_global_device_ids=true | all-gather | bytes 819200 | tf_op jit(solution)/shard_map/all_gather | solution.py:101
  111.5 3.4 fusion.38
  123.0 4.0 convolution_convert_fusion.2
  129.2 4.0 convolution_convert_fusion.3
  137.2 13.4 %reduce-scatter.9.cloned.1.call-done = bf16[32,2560]{1,0:T(8,128)(2,1)} async-done(((bf16[128,2560]{1,0:T(8,128)(2,1)}), bf16[32,2560]{1,0:T(8,128)(2,1)}) %reduce-scatter.9.cloned.1.call-update) | async-done | bytes 163856 | tf_op jit(solution)/shard_map/reduce_scatter | solution.py:166
  150.5 24.1 %reduce-scatter.7.cloned.1.call-done = bf16[32,2560]{1,0:T(8,128)(2,1)} async-done(((bf16[128,2560]{1,0:T(8,128)(2,1)}), bf16[32,2560]{1,0:T(8,128)(2,1)}) %reduce-scatter.7.cloned.1.call-update) | async-done | bytes 163856 | tf_op jit(solution)/shard_map/reduce_scatter | solution.py:166
  174.7 2.3 fusion.90
  178.8 16.5 %all_gather.36 = bf16[128,2560]{1,0:T(8,128)(2,1)S(1)} all-gather(bf16[32,2560]{1,0:T(8,128)(2,1)S(1)} %get-tuple-element.58), channel_id=1, replica_groups=mesh['section'=4,'tensor'=4,'dp'=2] {'tensor'}, dimensions={0}, use_global_device_ids=true | all-gather | bytes 819200 | tf_op jit(solution)/shard_map/all_gather | solution.py:100
  196.4 15.8 %all_gather.34 = bf16[128,2560]{1,0:T(8,128)(2,1)S(1)} all-gather(bf16[32,2560]{1,0:T(8,128)(2,1)S(1)} %get-tuple-element.59), channel_id=1, replica_groups=mesh['section'=4,'tensor'=4,'dp'=2] {'tensor'}, dimensions={0}, use_global_device_ids=true | all-gather | bytes 819200 | tf_op jit(solution)/shard_map/all_gather | solution.py:100
  214.8 3.0 collective-permute-start
  221.0 17.3 %all_gather.35 = bf16[128,2560]{1,0:T(8,128)(2,1)S(1)} all-gather(bf16[32,2560]{1,0:T(8,128)(2,1)S(1)} %broadcast_select_fusion), channel_id=1, replica_groups=mesh['section'=4,'tensor'=4,'dp'=2] {'tensor'}, dimensions={0}, use_global_device_ids=true | all-gather | bytes 819200 | tf_op jit(solution)/shard_map/all_gather | solution.py:101
  244.0 16.7 %all_gather.37 = bf16[128,2560]{1,0:T(8,128)(2,1)S(1)} all-gather(bf16[32,2560]{1,0:T(8,128)(2,1)S(1)} %bitcast_select_fusion), channel_id=1, replica_groups=mesh['section'=4,'tensor'=4,'dp'=2] {'tensor'}, dimensions={0}, use_global_device_ids=true | all-gather | bytes 819200 | tf_op jit(solution)/shard_map/all_gather | solution.py:101
  261.5 3.5 fusion.41
  272.2 2.0 convolution_convert_fusion
  277.3 4.0 convolution_convert_fusion.1
  281.2 3.2 fusion.189
  284.5 3.4 fusion.3
  289.9 2.7 pad_maximum_fusion.1
  298.0 3.4 pad_maximum_fusion
  302.5 19.2 %reduce-scatter.11.cloned.1.call-done = bf16[32,2560]{1,0:T(8,128)(2,1)} async-done(((bf16[128,2560]{1,0:T(8,128)(2,1)}), bf16[32,2560]{1,0:T(8,128)(2,1)}) %reduce-scatter.11.cloned.1.call-update) | async-done | bytes 163856 | tf_op jit(solution)/shard_map/reduce_scatter | solution.py:166
  323.2 31.0 %all-gather.3 = f32[8,2,2560]{2,1,0:T(2,128)S(1)} all-gather(f32[1,2,2560]{2,1,0:T(2,128)S(1)} %maximum_bitcast_fusion.7), channel_id=4, replica_groups=mesh['section'=4,'tensor'=4,'dp'=2] {'tensor','dp'}, dimensions={0}, use_global_device_ids=true | all-gather | bytes 184320 | tf_op jit(solution)/shard_map/all_gather | solution.py:214
  357.1 34.1 %reduce-scatter.17.cloned.1.call-done = bf16[2,256,2560]{2,1,0:T(8,128)(2,1)} async-done(((bf16[2,512,2560]{2,1,0:T(8,128)(2,1)}), bf16[2,256,2560]{2,1,0:T(8,128)(2,1)}) %reduce-scatter.17.cloned.1.call-update) | async-done | bytes 2621456 | tf_op jit(solution)/shard_map/reduce_scatter | solution.py:209
  391.2 82.6 %reduce-scatter.15.cloned.1.call-done = bf16[2,1280,640]{2,1,0:T(8,128)(2,1)} async-done(((bf16[2,2560,640]{2,1,0:T(8,128)(2,1)}), bf16[2,1280,640]{2,1,0:T(8,128)(2,1)}) %reduce-scatter.15.cloned.1.call-update) | async-done | bytes 3276816 | tf_op jit(solution)/shard_map/reduce_scatter | solution.py:206
  (320 shorter events, 62.4 us)
Async XLA Ops:
  7.2 28.0 %copy-start.1 = (bf16[2,2,1,1,32,2560]{5,4,3,2,1,0:T(8,128)(2,1)S(1)}, bf16[2,2,1,1,32,2560]{5,4,3,2,1,0:T(8,128)(2,1)}, u32[]{:S(2)}) copy-start(bf16[2,2,1,1,32,2560]{5,4,3,2,1,0:T(8,128)(2,1)} %param.6) | copy-start | bytes 1966084
  7.2 143.4 %reduce-scatter.9.cloned.1.call-start = ((), (), s32[]{:S(2)}) async-start(), calls=%async_computation.7 | async-start | bytes 819200 | tf_op jit(solution)/shard_map/reduce_scatter | solution.py:166
  7.2 84.4 %copy-start.88 = (f32[32]{0:T(128)}, f32[32]{0:T(128)S(1)}, u32[]{:S(2)}) copy-start(f32[32]{0:T(128)S(1)} %negate_power_fusion) | copy-start | bytes 388
  7.3 85.9 %copy-start.49 = (pred[128,128]{0,1:T(8,128)(4,1)}, pred[128,128]{0,1:T(8,128)(4,1)S(1)}, u32[]{:S(2)}) copy-start(pred[128,128]{0,1:T(8,128)(4,1)S(1)} %iota_compare_fusion) | copy-start | bytes 49156
  9.3 26.1 %copy-start.42 = (f32[2560]{0:T(1024)}, f32[2560]{0:T(1024)S(1)}, u32[]{:S(2)}) copy-start(f32[2560]{0:T(1024)S(1)} %get-tuple-element.53) | copy-start | bytes 30724
  10.1 82.3 %copy-start.45 = (f32[128,32]{0,1:T(8,128)}, f32[128,32]{0,1:T(8,128)S(1)}, u32[]{:S(2)}) copy-start(f32[128,32]{0,1:T(8,128)S(1)} %get-tuple-element.116) | copy-start | bytes 49156
  10.1 82.3 %copy-start.59 = (f32[128,32]{0,1:T(8,128)}, f32[128,32]{0,1:T(8,128)S(1)}, u32[]{:S(2)}) copy-start(f32[128,32]{0,1:T(8,128)S(1)} %get-tuple-element.115) | copy-start | bytes 49156
  35.1 58.4 %copy-start.63 = (bf16[128,512]{0,1:T(8,128)(2,1)}, bf16[128,512]{0,1:T(8,128)(2,1)S(1)}, u32[]{:S(2)}) copy-start(bf16[128,512]{0,1:T(8,128)(2,1)S(1)} %copy.65) | copy-start | bytes 393220
  35.2 40.7 %copy-start.92 = (f32[32]{0:T(128)}, f32[32]{0:T(128)S(1)}, u32[]{:S(2)}) copy-start(f32[32]{0:T(128)S(1)} %get-tuple-element.133) | copy-start | bytes 388
  35.2 40.7 %copy-start.94 = (f32[32]{0:T(128)}, f32[32]{0:T(128)S(1)}, u32[]{:S(2)}) copy-start(f32[32]{0:T(128)S(1)} %get-tuple-element.134) | copy-start | bytes 388
  127.0 47.6 %reduce-scatter.7.cloned.1.call-start = ((), (), s32[]{:S(2)}) async-start(), calls=%async_computation.6 | async-start | bytes 819200 | tf_op jit(solution)/shard_map/reduce_scatter | solution.py:166
  133.1 41.5 %copy-start.43 = (f32[2560]{0:T(1024)S(1)}, f32[2560]{0:T(1024)}, u32[]{:S(2)}) copy-start(f32[2560]{0:T(1024)} %copy-done.42) | copy-start | bytes 30724
  133.2 41.5 %copy-start.93 = (f32[32]{0:T(128)S(1)}, f32[32]{0:T(128)}, u32[]{:S(2)}) copy-start(f32[32]{0:T(128)} %copy-done.92) | copy-start | bytes 388
  133.2 41.5 %copy-start.95 = (f32[32]{0:T(128)S(1)}, f32[32]{0:T(128)}, u32[]{:S(2)}) copy-start(f32[32]{0:T(128)} %copy-done.94) | copy-start | bytes 388
  133.2 169.3 %reduce-scatter.13.cloned.1.call-start = ((), (), s32[]{:S(2)}) async-start(), calls=%async_computation.9 | async-start | bytes 819200 | tf_op jit(solution)/shard_map/reduce_scatter | solution.py:166
  174.7 20.7 %copy-start = (bf16[640,2560]{1,0:T(8,128)(2,1)S(1)}, bf16[640,2560]{1,0:T(8,128)(2,1)}, u32[]{:S(2)}) copy-start(bf16[640,2560]{1,0:T(8,128)(2,1)} %copy.69) | copy-start | bytes 9830404
  178.8 34.6 %copy-start.31 = (bf16[32,2560]{1,0:T(8,128)(2,1)}, bf16[32,2560]{1,0:T(8,128)(2,1)S(1)}, u32[]{:S(2)}) copy-start(bf16[32,2560]{1,0:T(8,128)(2,1)S(1)} %get-tuple-element.56) | copy-start | bytes 491524
  178.8 41.5 %copy-start.19 = (bf16[32,2560]{1,0:T(8,128)(2,1)}, bf16[32,2560]{1,0:T(8,128)(2,1)S(1)}, u32[]{:S(2)}) copy-start(bf16[32,2560]{1,0:T(8,128)(2,1)S(1)} %get-tuple-element.57) | copy-start | bytes 491524
  195.3 43.9 %slice-start.2 = ((s8[5242880]{0:T(1024)(128)(4,1)}), s8[1048576]{0:T(1024)(128)(4,1)S(1)}, s32[]{:S(2)}) async-start(s8[5242880]{0:T(1024)(128)(4,1)} %bitcast.495), calls=%async_computation.14 | async-start | bytes 2097152
  196.4 21.4 %copy-start.90 = (f32[32]{0:T(128)S(1)}, f32[32]{0:T(128)}, u32[]{:S(2)}) copy-start(f32[32]{0:T(128)} %copy-done.88) | copy-start | bytes 388
  196.4 21.6 %copy-start.50 = (pred[128,128]{0,1:T(8,128)(4,1)S(1)}, pred[128,128]{0,1:T(8,128)(4,1)}, u32[]{:S(2)}) copy-start(pred[128,128]{0,1:T(8,128)(4,1)} %copy-done.49) | copy-start | bytes 49156
  212.2 27.1 %slice-start.3 = ((s8[5242880]{0:T(1024)(128)(4,1)}), s8[4194304]{0:T(1024)(128)(4,1)S(1)}, s32[]{:S(2)}) async-start(s8[5242880]{0:T(1024)(128)(4,1)} %bitcast.495), calls=%async_computation.15 | async-start | bytes 8388608
  213.4 6.9 %collective-permute-start.1 = (bf16[32,2560]{1,0:T(8,128)(2,1)S(1)}, bf16[32,2560]{1,0:T(8,128)(2,1)S(1)}, u32[]{:S(2)}, u32[]{:S(2)}) collective-permute-start(bf16[32,2560]{1,0:T(8,128)(2,1)S(1)} %get-tuple-element.56), channel_id=1, source_target_pairs={{8,0},{16,8},{24,16},{9,1},{17,9},{25,17},{10,2},{18,10},{26,18},{... | collective-permute-start | bytes 491528 | tf_op jit(solution)/shard_map/ppermute | solution.py:17
  214.8 5.5 %collective-permute-start = (bf16[32,2560]{1,0:T(8,128)(2,1)S(1)}, bf16[32,2560]{1,0:T(8,128)(2,1)S(1)}, u32[]{:S(2)}, u32[]{:S(2)}) collective-permute-start(bf16[32,2560]{1,0:T(8,128)(2,1)S(1)} %get-tuple-element.57), channel_id=1, source_target_pairs={{0,8},{8,16},{16,24},{1,9},{9,17},{17,25},{2,10},{10,18},{18,26},{... | collective-permute-start | bytes 491528 | tf_op jit(solution)/shard_map/ppermute | solution.py:17
  218.4 23.0 %copy-start.84 = (f32[8,128]{1,0:T(8,128)}, f32[8,128]{1,0:T(8,128)S(1)}, u32[]{:S(2)}) copy-start(f32[8,128]{1,0:T(8,128)S(1)} %fusion.53) | copy-start | bytes 12292
  274.2 47.5 %reduce-scatter.11.cloned.1.call-start = ((), (), s32[]{:S(2)}) async-start(), calls=%async_computation.8 | async-start | bytes 819200 | tf_op jit(solution)/shard_map/reduce_scatter | solution.py:166
  284.4 106.8 %reduce-scatter.17.cloned.1.call-start = ((), (), s32[]{:S(2)}) async-start(), calls=%async_computation.11 | async-start | bytes 7864320 | tf_op jit(solution)/shard_map/reduce_scatter | solution.py:209
  292.6 181.2 %reduce-scatter.15.cloned.1.call-start = ((), (), s32[]{:S(2)}) async-start(), calls=%async_computation.10 | async-start | bytes 9830400 | tf_op jit(solution)/shard_map/reduce_scatter | solution.py:206
  301.4 21.6 %copy-start.75 = (f32[2560]{0:T(1024)S(1)}, f32[2560]{0:T(1024)}, u32[]{:S(2)}) copy-start(f32[2560]{0:T(1024)} %get-tuple-element.47) | copy-start | bytes 30724
  301.4 21.7 %copy-start.74 = (f32[2560]{0:T(1024)S(1)}, f32[2560]{0:T(1024)}, u32[]{:S(2)}) copy-start(f32[2560]{0:T(1024)} %get-tuple-element.38) | copy-start | bytes 30724
  301.5 53.4 %copy-start.22 = (bf16[32,2560]{1,0:T(8,128)(2,1)S(1)}, bf16[32,2560]{1,0:T(8,128)(2,1)}, u32[]{:S(2)}) copy-start(bf16[32,2560]{1,0:T(8,128)(2,1)} %copy-done.21) | copy-start | bytes 491524
  301.5 53.4 %copy-start.24 = (bf16[32,2560]{1,0:T(8,128)(2,1)S(1)}, bf16[32,2560]{1,0:T(8,128)(2,1)}, u32[]{:S(2)}) copy-start(bf16[32,2560]{1,0:T(8,128)(2,1)} %copy-done.23) | copy-start | bytes 491524
  (80 other events, 446.7 us)
Sparse Core Ops, SparseCore 0:
  127.1 23.3 reduce-scatter.8
  153.4 21.2 reduce-scatter.6
  274.4 23.2 reduce-scatter.12
  300.4 21.2 reduce-scatter.10
  324.4 66.7 reduce-scatter.16
  393.9 79.8 reduce-scatter.14
